TPU v7x, 16 devices: a whole 2x2x2 slice. The times are simulated.
16 devices in a mesh: col: 4 (over z, y), row: 4 (over x, core).
Axes of the slice: x: 2, y: 2, z: 2, core: 2. Of those that a mesh axis runs over, the one named last changes fastest.
Arguments:
- x_in: bfloat16 [1, 96, 768, 512], P(None, 'row', 'col')
- a_pre: bfloat16 [1, 96, 768, 512], P(None, 'row', 'col')
- g_out: bfloat16 [1, 96, 768, 512], P(None, 'row', 'col')
- w_one: bfloat16 [3, 3, 512, 512], replicated
- w_two: bfloat16 [3, 3, 512, 512], replicated
Outputs:
- output 1: bfloat16 [1, 96, 768, 512], P(None, 'row', 'col')
- output 2: float32 [3, 3, 512, 512], replicated
- output 3: float32 [3, 3, 512, 512], replicated
All inputs are finite; a program needn't handle non-finite values.
Results may differ from a plain program's by a relative error of at most 0.001.
Values are sent between devices in bfloat16 or wider.
A program may use at most 1 GiB of HBM per device.

v0:
```python
import jax
import jax.numpy as jnp
from jax import lax
from jax.sharding import PartitionSpec as P

DATA_DIMS = ("NHWC", "HWOI", "NHWC")


def gelu_slope(pre_act):
    tanh_scale = 0.7978845608028654
    cube_coef = 0.044715
    tanh_val = jnp.tanh(tanh_scale * (pre_act + cube_coef * pre_act * pre_act * pre_act))
    return 0.5 * (1.0 + tanh_val) + 0.5 * pre_act * (1.0 - tanh_val * tanh_val) * tanh_scale * (1.0 + 3.0 * cube_coef * pre_act * pre_act)


def conv_valid(lhs_arr, rhs_arr):
    return lax.conv_general_dilated(lhs_arr, rhs_arr, (1, 1), "VALID", dimension_numbers=DATA_DIMS, preferred_element_type=jnp.float32)


def tap_grads(tile_in, grad_wide):
    row_count = tile_in.shape[1]
    col_count = tile_in.shape[2]
    return jnp.stack([jnp.stack([jnp.einsum("bhwi,bhwo->io", tile_in, grad_wide[:, 2 - tap_row:2 - tap_row + row_count, 2 - tap_col:2 - tap_col + col_count], preferred_element_type=jnp.float32) for tap_col in range(3)]) for tap_row in range(3)])


def shift_pairs(count):
    forward_pairs = [(source, source + 1) for source in range(count - 1)]
    backward_pairs = [(source + 1, source) for source in range(count - 1)]
    return forward_pairs, backward_pairs


def solution(mesh):
    row_down, row_up = shift_pairs(mesh.shape["row"])
    col_down, col_up = shift_pairs(mesh.shape["col"])

    def add_halo(tile):
        from_above = lax.ppermute(tile[:, -1:], "row", row_down)
        from_below = lax.ppermute(tile[:, :1], "row", row_up)
        tall = jnp.concatenate([from_above, tile, from_below], axis=1)
        from_left = lax.ppermute(tall[:, :, -1:], "col", col_down)
        from_right = lax.ppermute(tall[:, :, :1], "col", col_up)
        return jnp.concatenate([from_left, tall, from_right], axis=2)

    def local_step(x_tile, a_tile, g_tile, w_one, w_two):
        a_val = a_tile.astype(jnp.float32)
        z_act = jax.nn.gelu(a_val, approximate=True).astype(jnp.bfloat16)
        g_wide = add_halo(g_tile)
        d_z = conv_valid(g_wide, w_two[::-1, ::-1])
        w2_part = tap_grads(z_act, g_wide)
        d_a = (d_z * gelu_slope(a_val)).astype(jnp.bfloat16)
        grad_wide = add_halo(d_a)
        d_x = (conv_valid(grad_wide, w_one[::-1, ::-1]) + g_tile.astype(jnp.float32)).astype(jnp.bfloat16)
        w1_part = tap_grads(x_tile, grad_wide)
        d_w1, d_w2 = lax.psum((w1_part, w2_part), ("row", "col"))
        return d_x, d_w1, d_w2

    tile_spec = P(None, "row", "col", None)
    return jax.shard_map(local_step, mesh=mesh, in_specs=(tile_spec, tile_spec, tile_spec, P(), P()), out_specs=(tile_spec, P(), P()), check_vma=False)
```

profile of v0, /device:TPU:0, one launch (start us, length us, event | category | flops | bytes accessed | tf_op | source)
XLA Modules:
  0.0 429.3 jit_solution(9357642961848769118)
XLA Ops:
  13.1 8.7 %fusion.104 = f32[1,512,512]{2,1,0:T(8,128)} fusion(bf16[1,24,192,512]{3,2,1,0:T(8,128)(2,1)} %param.7, bf16[1,24,192,512]{3,2,1,0:T(8,128)(2,1)} %param.6), kind=kOutput, calls=%fused_computation.132 | convolution fusion | flops 2439512064 | bytes 10485760 | tf_op jit(solution)/shard_map/bhwi,bhwo->io/dot_general | solution.py:23
  29.4 6.1 %fusion.141 = f32[1,512,512]{2,1,0:T(8,128)} fusion(bf16[1,24,192,512]{3,2,1,0:T(8,128)(2,1)S(1)} %bitcast.270, bf16[1,1,192,512]{3,2,1,0:T(8,128)(2,1)S(1)} %collective-permute-done, bf16[1,24,192,512]{3,2,1,0:T(8,128)(2,1)S(1)} %bitcast.276), kind=kOutput, calls=%fused_computation.143 | convolution fusion | flops 2441871360 | bytes 10682368 | tf_op jit(solution)/shard_map/bhwi,bhwo->io/dot_general | solution.py:23
  35.6 6.0 %fusion.135 = f32[1,512,512]{2,1,0:T(8,128)} fusion(bf16[1,1,192,512]{3,2,1,0:T(8,128)(2,1)S(1)} %collective-permute-done.1, bf16[1,24,192,512]{3,2,1,0:T(8,128)(2,1)S(1)} %bitcast.270, bf16[1,24,192,512]{3,2,1,0:T(8,128)(2,1)S(1)} %bitcast.276), kind=kOutput, calls=%fused_computation.141 | convolution fusion | flops 2441871360 | bytes 10682368 | tf_op jit(solution)/shard_map/bhwi,bhwo->io/dot_general | solution.py:23
  47.9 9.0 %reshape.104 = bf16[26,1,8,25,512]{4,3,2,0,1:T(8,128)(2,1)} reshape(bf16[26,1,200,512]{3,2,0,1:T(8,128)(2,1)} %pad) | data formatting | bytes 10649600 | tf_op jit(solution)/shard_map/conv_general_dilated | solution.py:17
  56.9 7.1 %copy.10 = bf16[26,1,8,25,512]{4,2,3,0,1:T(8,128)(2,1)S(1)} copy(bf16[26,1,8,25,512]{4,3,2,0,1:T(8,128)(2,1)} %reshape.104) | data formatting | bytes 10649600 | tf_op jit(solution)/shard_map/conv_general_dilated | solution.py:17
  64.1 25.7 %broadcast_select_fusion.1 = f32[24,8,25,512]{3,1,2,0:T(8,128)} fusion(pred[8,25]{0,1:T(8,128)(4,1)S(1)} %copy-done.6, bf16[3,3,512,512]{3,2,1,0:T(8,128)(2,1)S(1)} %bitcast.280, bf16[26,1,7,2,512]{4,2,3,0,1:T(8,128)(2,1)S(1)} %slice.118, bf16[26,1,8,25,512]{4,2,3,0,1:T(8,128)(2,1)S(1)} %copy.10), kind=kOutput, calls=%fused_computation.56 | convolution fusion | flops 22668951552 | bytes 20246728 | tf_op jit(solution)/shard_map/conv_general_dilated | solution.py:17
  89.8 9.5 %copy.11 = f32[24,8,25,512]{3,0,2,1:T(8,128)S(1)} copy(f32[24,8,25,512]{3,1,2,0:T(8,128)} %broadcast_select_fusion.1) | data formatting | bytes 19660800 | tf_op jit(solution)/shard_map/conv_general_dilated | solution.py:17
  104.2 11.3 %fusion.9 = bf16[1,24,192,512]{3,2,1,0:T(8,128)(2,1)S(1)} fusion(bf16[1,24,192,512]{3,2,1,0:T(8,128)(2,1)} %param.6, f32[24,1,192,512]{3,0,2,1:T(8,128)} %slice.119), kind=kLoop, calls=%fused_computation.21 | loop fusion | flops 47185920 | bytes 18874368 | tf_op jit(solution)/shard_map/convert_element_type | solution.py:50
  124.6 5.9 %fusion.138 = f32[1,512,512]{2,1,0:T(8,128)S(1)} fusion(bf16[1,26,1,512]{3,2,1,0:T(2,128)(2,1)S(1)} %collective-permute-done.3, bf16[1,26,192,512]{3,2,1,0:T(8,128)(2,1)S(1)} %bitcast.274, bf16[1,24,192,512]{3,2,1,0:T(8,128)(2,1)S(1)} %bitcast.278), kind=kOutput, calls=%fused_computation.142 | convolution fusion | flops 2448949248 | bytes 10905600 | tf_op jit(solution)/shard_map/bhwi,bhwo->io/dot_general | solution.py:23
  130.5 5.8 %fusion.144 = f32[1,512,512]{2,1,0:T(8,128)S(1)} fusion(bf16[1,26,192,512]{3,2,1,0:T(8,128)(2,1)S(1)} %bitcast.274, bf16[1,26,1,512]{3,2,1,0:T(2,128)(2,1)S(1)} %collective-permute-done.2, bf16[1,24,192,512]{3,2,1,0:T(8,128)(2,1)S(1)} %bitcast.278), kind=kOutput, calls=%fused_computation.144 | convolution fusion | flops 2448949248 | bytes 10905600 | tf_op jit(solution)/shard_map/bhwi,bhwo->io/dot_general | solution.py:23
  136.7 6.3 %fusion.147 = f32[1,512,512]{2,1,0:T(8,128)S(1)} fusion(bf16[1,26,192,512]{3,2,1,0:T(8,128)(2,1)S(1)} %bitcast.274, bf16[1,26,1,512]{3,2,1,0:T(2,128)(2,1)S(1)} %collective-permute-done.3, bf16[1,24,192,512]{3,2,1,0:T(8,128)(2,1)S(1)} %bitcast.278), kind=kOutput, calls=%fused_computation.145 | convolution fusion | flops 2448949248 | bytes 10905600 | tf_op jit(solution)/shard_map/bhwi,bhwo->io/dot_general | solution.py:23
  143.0 5.9 %fusion.150 = f32[1,512,512]{2,1,0:T(8,128)S(1)} fusion(bf16[1,26,192,512]{3,2,1,0:T(8,128)(2,1)S(1)} %bitcast.274, bf16[1,26,1,512]{3,2,1,0:T(2,128)(2,1)S(1)} %collective-permute-done.3, bf16[1,24,192,512]{3,2,1,0:T(8,128)(2,1)S(1)} %bitcast.278), kind=kOutput, calls=%fused_computation.146 | convolution fusion | flops 2448949248 | bytes 10905600 | tf_op jit(solution)/shard_map/bhwi,bhwo->io/dot_general | solution.py:23
  148.9 6.0 %fusion.153 = f32[1,512,512]{2,1,0:T(8,128)S(1)} fusion(bf16[1,26,192,512]{3,2,1,0:T(8,128)(2,1)S(1)} %bitcast.274, bf16[1,26,1,512]{3,2,1,0:T(2,128)(2,1)S(1)} %collective-permute-done.2, bf16[1,24,192,512]{3,2,1,0:T(8,128)(2,1)S(1)} %bitcast.278), kind=kOutput, calls=%fused_computation.147 | convolution fusion | flops 2448949248 | bytes 10905600 | tf_op jit(solution)/shard_map/bhwi,bhwo->io/dot_general | solution.py:23
  154.9 5.8 %fusion.156 = f32[1,512,512]{2,1,0:T(8,128)S(1)} fusion(bf16[1,26,192,512]{3,2,1,0:T(8,128)(2,1)S(1)} %bitcast.274, bf16[1,26,1,512]{3,2,1,0:T(2,128)(2,1)S(1)} %collective-permute-done.2, bf16[1,24,192,512]{3,2,1,0:T(8,128)(2,1)S(1)} %bitcast.278), kind=kOutput, calls=%fused_computation.148 | convolution fusion | flops 2448949248 | bytes 10905600 | tf_op jit(solution)/shard_map/bhwi,bhwo->io/dot_general | solution.py:23
  203.5 6.1 %maximum_bitcast_fusion.1 = bf16[26,1,194,512]{3,2,0,1:T(8,128)(2,1)S(1)} fusion(bf16[1,26,1,512]{3,2,1,0:T(2,128)(2,1)S(1)} %collective-permute-done.7, bf16[1,1,192,512]{3,2,1,0:T(8,128)(2,1)S(1)} %collective-permute-done.5, bf16[1,24,192,512]{3,2,1,0:T(8,128)(2,1)} %copy-done, bf16[1,1,192,512]{3,2,1,0:T(8,128)(2,1)S(1)} %collective-permute-done.4, ...), kind=kLoop, calls=%fused_computation.52 | loop fusion | flops 25825280 | bytes 10330112 | tf_op jit(solution)/shard_map/concatenate | solution.py:42
  212.4 8.7 %reshape.109 = bf16[26,1,8,25,512]{4,3,2,0,1:T(8,128)(2,1)} reshape(bf16[26,1,200,512]{3,2,0,1:T(8,128)(2,1)} %pad.2) | data formatting | bytes 10649600 | tf_op jit(solution)/shard_map/conv_general_dilated | solution.py:17
  221.1 7.1 %copy.14 = bf16[26,1,8,25,512]{4,2,3,0,1:T(8,128)(2,1)S(1)} copy(bf16[26,1,8,25,512]{4,3,2,0,1:T(8,128)(2,1)} %reshape.109) | data formatting | bytes 10649600 | tf_op jit(solution)/shard_map/conv_general_dilated | solution.py:17
  228.3 25.9 %broadcast_select_fusion = f32[24,8,25,512]{3,1,2,0:T(8,128)} fusion(pred[8,25]{0,1:T(8,128)(4,1)S(1)} %copy-done.7, bf16[3,3,512,512]{3,2,1,0:T(8,128)(2,1)S(1)} %bitcast.282, bf16[26,1,7,2,512]{4,2,3,0,1:T(8,128)(2,1)S(1)} %slice.122, bf16[26,1,8,25,512]{4,2,3,0,1:T(8,128)(2,1)S(1)} %copy.14), kind=kOutput, calls=%fused_computation.55 | convolution fusion | flops 22668951552 | bytes 20246728 | tf_op jit(solution)/shard_map/conv_general_dilated | solution.py:17
  254.3 9.5 %copy.15 = f32[24,8,25,512]{3,0,2,1:T(8,128)S(1)} copy(f32[24,8,25,512]{3,1,2,0:T(8,128)} %broadcast_select_fusion) | data formatting | bytes 19660800 | tf_op jit(solution)/shard_map/conv_general_dilated | solution.py:17
  263.7 7.9 %fusion.18 = bf16[1,24,192,512]{3,1,2,0:T(8,128)(2,1)} fusion(f32[24,1,200,512]{3,0,2,1:T(8,128)S(1)} %bitcast.268, bf16[1,24,192,512]{3,2,1,0:T(8,128)(2,1)} %param.7), kind=kLoop, calls=%fused_computation.31 | loop fusion | flops 7077888 | bytes 18874368 | tf_op jit(solution)/shard_map/convert_element_type | solution.py:52
  271.7 6.1 %copy.17 = bf16[1,24,192,512]{3,2,1,0:T(8,128)(2,1)} copy(bf16[1,24,192,512]{3,1,2,0:T(8,128)(2,1)} %fusion.18) | data formatting | bytes 9437184
  277.8 126.3 %all-reduce.3.cloned.1.call-done = (f32[3,3,512,512]{2,3,1,0:T(8,128)}, f32[3,3,512,512]{3,2,1,0:T(8,128)}) async-done(((f32[3,3,512,512]{2,3,1,0:T(8,128)}, f32[3,3,512,512]{3,2,1,0:T(8,128)}), (f32[3,3,512,512]{2,3,1,0:T(8,128)}, f32[3,3,512,512]{3,2,1,0:T(8,128)})) %all-reduce.3.cloned.1.call-update) | async-done | bytes 18874384 | tf_op jit(solution)/shard_map/psum | solution.py:54
  404.1 9.6 %copy.18 = f32[3,3,512,512]{3,2,1,0:T(8,128)} copy(f32[3,3,512,512]{2,3,1,0:T(8,128)} %get-tuple-element.9) | data formatting | bytes 18874368
  413.7 8.5 %copy.28 = f32[3,3,512,512]{3,2,1,0:T(8,128)} copy(f32[3,3,512,512]{3,2,1,0:T(8,128)} %get-tuple-element.27) | data formatting | bytes 18874368
  (98 shorter events, 79.6 us)
Async XLA Ops:
  7.2 397.0 %all-reduce.3.cloned.1.call-start = ((), (), s32[]{:S(2)}) async-start(), calls=%async_computation | async-start | bytes 37748736 | tf_op jit(solution)/shard_map/psum | solution.py:54
  8.3 14.3 %collective-permute-start.1 = (bf16[1,1,192,512]{3,2,1,0:T(8,128)(2,1)S(1)}, bf16[1,1,192,512]{3,2,1,0:T(8,128)(2,1)S(1)}, u32[]{:S(2)}, u32[]{:S(2)}) collective-permute-start(bf16[1,1,192,512]{3,2,1,0:T(8,128)(2,1)S(1)} %get-tuple-element.19), channel_id=1, source_target_pairs={{1,0},{2,1},{3,2},{5,4},{6,5},{7,6},{9,8},{10,9},{11,10},{13,12},{... | collective-permute-start | bytes 589832 | tf_op jit(solution)/shard_map/ppermute | solution.py:38
  9.6 12.4 %slice-start = ((s8[4718592]{0:T(1024)(128)(4,1)}), s8[4194304]{0:T(1024)(128)(4,1)S(1)}, s32[]{:S(2)}) async-start(s8[4718592]{0:T(1024)(128)(4,1)} %bitcast.269), calls=%async_computation.1 | async-start | bytes 8388608
  9.6 12.3 %slice-start.1 = ((s8[4718592]{0:T(1024)(128)(4,1)}), s8[524288]{0:T(1024)(128)(4,1)S(1)}, s32[]{:S(2)}) async-start(s8[4718592]{0:T(1024)(128)(4,1)} %bitcast.269), calls=%async_computation.2 | async-start | bytes 1048576
  9.6 12.3 %collective-permute-start = (bf16[1,1,192,512]{3,2,1,0:T(8,128)(2,1)S(1)}, bf16[1,1,192,512]{3,2,1,0:T(8,128)(2,1)S(1)}, u32[]{:S(2)}, u32[]{:S(2)}) collective-permute-start(bf16[1,1,192,512]{3,2,1,0:T(8,128)(2,1)S(1)} %get-tuple-element.20), channel_id=1, source_target_pairs={{0,1},{1,2},{2,3},{4,5},{5,6},{6,7},{8,9},{9,10},{10,11},{12,13},{... | collective-permute-start | bytes 589832 | tf_op jit(solution)/shard_map/ppermute | solution.py:37
  21.9 7.5 %slice-start.6 = ((s8[4718592]{0:T(1024)(128)(4,1)}), s8[4194304]{0:T(1024)(128)(4,1)S(1)}, s32[]{:S(2)}) async-start(s8[4718592]{0:T(1024)(128)(4,1)} %bitcast.275), calls=%async_computation.7 | async-start | bytes 8388608
  21.9 7.5 %slice-start.7 = ((s8[4718592]{0:T(1024)(128)(4,1)}), s8[524288]{0:T(1024)(128)(4,1)S(1)}, s32[]{:S(2)}) async-start(s8[4718592]{0:T(1024)(128)(4,1)} %bitcast.275), calls=%async_computation.8 | async-start | bytes 1048576
  22.6 19.0 %copy-start.1 = (bf16[1,26,192,512]{3,2,1,0:T(8,128)(2,1)}, bf16[1,26,192,512]{3,2,1,0:T(8,128)(2,1)S(1)}, u32[]{:S(2)}) copy-start(bf16[1,26,192,512]{3,2,1,0:T(8,128)(2,1)S(1)} %constant_dynamic-update-slice_fusion) | copy-start | bytes 15335428
  22.7 18.9 %collective-permute-start.2 = (bf16[1,26,1,512]{3,2,1,0:T(2,128)(2,1)S(1)}, bf16[1,26,1,512]{3,2,1,0:T(2,128)(2,1)S(1)}, u32[]{:S(2)}, u32[]{:S(2)}) collective-permute-start(bf16[1,26,1,512]{3,2,1,0:T(2,128)(2,1)S(1)} %get-tuple-element.15), channel_id=1, source_target_pairs={{0,4},{4,8},{8,12},{1,5},{5,9},{9,13},{2,6},{6,10},{10,14},{3,7},{... | collective-permute-start | bytes 79880 | tf_op jit(solution)/shard_map/ppermute | solution.py:40
  27.9 13.7 %collective-permute-start.3 = (bf16[1,26,1,512]{3,2,1,0:T(2,128)(2,1)S(1)}, bf16[1,26,1,512]{3,2,1,0:T(2,128)(2,1)S(1)}, u32[]{:S(2)}, u32[]{:S(2)}) collective-permute-start(bf16[1,26,1,512]{3,2,1,0:T(2,128)(2,1)S(1)} %get-tuple-element.16), channel_id=1, source_target_pairs={{4,0},{8,4},{12,8},{5,1},{9,5},{13,9},{6,2},{10,6},{14,10},{7,3},{... | collective-permute-start | bytes 79880 | tf_op jit(solution)/shard_map/ppermute | solution.py:41
  47.9 16.2 %slice-start.10 = ((s8[4718592]{0:T(1024)(128)(4,1)}), s8[524288]{0:T(1024)(128)(4,1)S(1)}, s32[]{:S(2)}) async-start(s8[4718592]{0:T(1024)(128)(4,1)} %bitcast.279), calls=%async_computation.11 | async-start | bytes 1048576
  56.9 7.2 %slice-start.11 = ((s8[4718592]{0:T(1024)(128)(4,1)}), s8[4194304]{0:T(1024)(128)(4,1)S(1)}, s32[]{:S(2)}) async-start(s8[4718592]{0:T(1024)(128)(4,1)} %bitcast.279), calls=%async_computation.12 | async-start | bytes 8388608
  56.9 7.2 %copy-start.6 = (pred[8,25]{0,1:T(8,128)(4,1)S(1)}, pred[8,25]{0,1:T(8,128)(4,1)}, u32[]{:S(2)}) copy-start(pred[8,25]{0,1:T(8,128)(4,1)} %constant.18) | copy-start | bytes 604
  99.3 21.7 %slice-start.2 = ((s8[4718592]{0:T(1024)(128)(4,1)}), s8[4194304]{0:T(1024)(128)(4,1)S(1)}, s32[]{:S(2)}) async-start(s8[4718592]{0:T(1024)(128)(4,1)} %bitcast.271), calls=%async_computation.3 | async-start | bytes 8388608
  104.2 16.8 %slice-start.3 = ((s8[4718592]{0:T(1024)(128)(4,1)}), s8[524288]{0:T(1024)(128)(4,1)S(1)}, s32[]{:S(2)}) async-start(s8[4718592]{0:T(1024)(128)(4,1)} %bitcast.271), calls=%async_computation.4 | async-start | bytes 1048576
  115.5 61.8 %copy-start = (bf16[1,24,192,512]{3,2,1,0:T(8,128)(2,1)}, bf16[1,24,192,512]{3,2,1,0:T(8,128)(2,1)S(1)}, u32[]{:S(2)}) copy-start(bf16[1,24,192,512]{3,2,1,0:T(8,128)(2,1)S(1)} %fusion.9) | copy-start | bytes 14155780
  116.4 49.9 %collective-permute-start.4 = (bf16[1,1,192,512]{3,2,1,0:T(8,128)(2,1)}, bf16[1,1,192,512]{3,2,1,0:T(8,128)(2,1)S(1)}, u32[]{:S(2)}, u32[]{:S(2)}) collective-permute-start(bf16[1,1,192,512]{3,2,1,0:T(8,128)(2,1)} %get-tuple-element.17), channel_id=1, source_target_pairs={{0,1},{1,2},{2,3},{4,5},{5,6},{6,7},{8,9},{9,10},{10,11},{12,13},{... | collective-permute-start | bytes 589832 | tf_op jit(solution)/shard_map/ppermute | solution.py:37
  119.2 47.1 %collective-permute-start.5 = (bf16[1,1,192,512]{3,2,1,0:T(8,128)(2,1)}, bf16[1,1,192,512]{3,2,1,0:T(8,128)(2,1)S(1)}, u32[]{:S(2)}, u32[]{:S(2)}) collective-permute-start(bf16[1,1,192,512]{3,2,1,0:T(8,128)(2,1)} %get-tuple-element.18), channel_id=1, source_target_pairs={{1,0},{2,1},{3,2},{5,4},{6,5},{7,6},{9,8},{10,9},{11,10},{13,12},{... | collective-permute-start | bytes 589832 | tf_op jit(solution)/shard_map/ppermute | solution.py:38
  154.9 5.8 %copy-start.3 = (f32[1,512,512]{2,1,0:T(8,128)S(1)}, f32[1,512,512]{2,1,0:T(8,128)}, u32[]{:S(2)}) copy-start(f32[1,512,512]{2,1,0:T(8,128)} %fusion.104) | copy-start | bytes 3145732
  166.4 10.8 %collective-permute-start.6 = (bf16[1,26,1,512]{3,2,1,0:T(2,128)(2,1)S(1)}, bf16[1,26,1,512]{3,2,1,0:T(2,128)(2,1)S(1)}, u32[]{:S(2)}, u32[]{:S(2)}) collective-permute-start(bf16[1,26,1,512]{3,2,1,0:T(2,128)(2,1)S(1)} %get-tuple-element.13), channel_id=1, source_target_pairs={{0,4},{4,8},{8,12},{1,5},{5,9},{9,13},{2,6},{6,10},{10,14},{3,7},{... | collective-permute-start | bytes 79880 | tf_op jit(solution)/shard_map/ppermute | solution.py:40
  170.7 6.6 %collective-permute-start.7 = (bf16[1,26,1,512]{3,2,1,0:T(2,128)(2,1)S(1)}, bf16[1,26,1,512]{3,2,1,0:T(2,128)(2,1)S(1)}, u32[]{:S(2)}, u32[]{:S(2)}) collective-permute-start(bf16[1,26,1,512]{3,2,1,0:T(2,128)(2,1)S(1)} %get-tuple-element.14), channel_id=1, source_target_pairs={{4,0},{8,4},{12,8},{5,1},{9,5},{13,9},{6,2},{10,6},{14,10},{7,3},{... | collective-permute-start | bytes 79880 | tf_op jit(solution)/shard_map/ppermute | solution.py:41
  212.4 15.9 %slice-start.12 = ((s8[4718592]{0:T(1024)(128)(4,1)}), s8[524288]{0:T(1024)(128)(4,1)S(1)}, s32[]{:S(2)}) async-start(s8[4718592]{0:T(1024)(128)(4,1)} %bitcast.281), calls=%async_computation.13 | async-start | bytes 1048576
  221.1 7.2 %slice-start.13 = ((s8[4718592]{0:T(1024)(128)(4,1)}), s8[4194304]{0:T(1024)(128)(4,1)S(1)}, s32[]{:S(2)}) async-start(s8[4718592]{0:T(1024)(128)(4,1)} %bitcast.281), calls=%async_computation.14 | async-start | bytes 8388608
  221.1 7.2 %copy-start.7 = (pred[8,25]{0,1:T(8,128)(4,1)S(1)}, pred[8,25]{0,1:T(8,128)(4,1)}, u32[]{:S(2)}) copy-start(pred[8,25]{0,1:T(8,128)(4,1)} %constant.18) | copy-start | bytes 604
  (7 other events, 34.6 us)
Sparse Core Ops, SparseCore 0:
  203.6 200.4 all-reduce.2
where the time goes:
time: 434 us; the launch traced here: 429 us
  matrix products  133 us (31%)
  waiting for transfers between devices  126 us (29%)
  local copies, waits for them, and re-layouts  89.3 us (21%)
  other arithmetic  44.3 us (10%)
  starting transfers between devices  21.7 us (5%)
  between operations  14.8 us (3%)
    psum x1, waiting for transfers between devices, local_step(): d_w1, d_w2 = lax.psum((w1_part, w2_part), ('row', 'col'))  126 us
    dot_general x18, matrix products, tap_grads(): jnp.einsum('bhwi,bhwo->io', tile_in, grad_wide[:, 2 - tap_row:2 - tap_row...  81.2 us
    conv_general_dilated x9, local copies, waits for them, and re-layouts, conv_valid(): lax.conv_general_dilated(lhs_arr, rhs_arr, (1, 1), 'VALID', dimension_num...  55.9 us
    conv_general_dilated x2, matrix products, conv_valid(): lax.conv_general_dilated(lhs_arr, rhs_arr, (1, 1), 'VALID', dimension_num...  51.6 us
    unnamed x49, local copies, waits for them, and re-layouts  25.9 us
    concatenate x3, other arithmetic, add_halo(): return jnp.concatenate([from_left, tall, from_right], axis=2)  12.8 us
    another operation x6, other arithmetic, tap_grads(): jnp.stack([jnp.stack([jnp.einsum('bhwi,bhwo->io', tile_in, grad_wide[:, 2...  12.2 us
    convert_element_type x1, other arithmetic, local_step(): d_a = (d_z * gelu_slope(a_val)).astype(jnp.bfloat16)  11.3 us
  transfers between devices with their start and end apart: 9, of which 1 were waited for; matrix products, arithmetic and copies ran while one was open for 34% of the time, Pallas kernels for 0%

commit v1 on v0

v1 whole, which is shorter than its diff:
```python
import functools

import jax
import jax.numpy as jnp
from jax import lax
from jax.experimental import pallas as pl
from jax.experimental.pallas import tpu as pltpu
from jax.sharding import PartitionSpec as P

MESH = pl.DeviceIdType.MESH
F32 = jnp.float32
BF16 = jnp.bfloat16
ROWS, COLS, CH = 24, 192, 512
PIX = ROWS * COLS
GROUP = 4
GPIX = GROUP * COLS
NGROUP = ROWS // GROUP
HALVES = (256, 128, 64, 32)
SLOTS = None


def build_slots(tap=2.7, first=11.0, shift=4.5, group=4.6, xpose=3.5, dgroup=4.2, rate=46.0, lat=2.6, margin=0.0):
    msg = {1: 0.262144e6, 2: 0.131072e6, 3: 0.065536e6}
    link_free = [0.0, 0.0, 0.0]
    arrive = {}
    done_prev = {}

    def send(now, w, t, s):
        if s == 0 or s == 7:
            arrive[(w, t, s)] = now + 2.2
            return
        level = s if s <= 3 else 7 - s
        dim = (t + level - 1) % 3
        begin = max(now, link_free[dim])
        link_free[dim] = begin + msg[level] / (rate * 1e3)
        arrive[(w, t, s)] = link_free[dim] + lat

    steps = []
    for i in range(9):
        steps.append((tap + (shift if i == 3 else 0.0), (0, i)))
    for gi in range(NGROUP):
        steps.append((group, None))
    for i in range(9):
        steps.append((tap + (shift if i == 3 else 0.0) + (xpose if i == 0 else 0.0), (1, i)))
    for gi in range(NGROUP):
        steps.append((dgroup, None))
    now = first
    slots = []
    for length, made in steps:
        if made is not None and made[0] == 1:
            while any(k[:2] == (0, made[1]) for k in arrive):
                v, (w, t, s) = min((v, k) for k, v in arrive.items())
                del arrive[(w, t, s)]
                now = max(now, v) + 0.25
                slots[-1].append((w, t, s))
                if s < 7:
                    send(now, w, t, s + 1)
        now += length
        here = []
        if made is not None:
            send(now, made[0], made[1], 0)
        while True:
            ready = sorted((k[2] > 3, v, k) for k, v in arrive.items() if v + margin <= now)
            if not ready:
                break
            w, t, s = ready[0][2]
            del arrive[(w, t, s)]
            here.append((w, t, s))
            now += 0.15
            if s < 7:
                send(now, w, t, s + 1)
        slots.append(here)
    tail = []
    while arrive:
        v, (w, t, s) = min((v, k) for k, v in arrive.items())
        del arrive[(w, t, s)]
        now = max(now, v) + 0.2
        tail.append((w, t, s))
        if s < 7:
            send(now, w, t, s + 1)
    slots.append(tail)
    return slots, now


def gelu_val(a):
    return a * (0.5 * (1.0 + jnp.tanh(0.7978845608028654 * (a + 0.044715 * (a * a * a)))))


def gelu_slope(a):
    t = jnp.tanh(0.7978845608028654 * (a + 0.044715 * a * a * a))
    return 0.5 * (1.0 + t) + 0.5 * a * (1.0 - t * t) * 0.7978845608028654 * (1.0 + 3.0 * 0.044715 * a * a)


def order_of(i):
    plane = (i // 3 + 1) % 3
    row = (i % 3 + 1) % 3
    return plane, row, (2 - row) * 3 + (2 - plane)


def kernel(slots, x_ref, a_ref, g_ref, w1_ref, w2_ref, dx_ref, dw1_ref, dw2_ref,
           part, full, r0, r1, r2, r3, lhs_t, gs, wbuf, stage, edge_out, edge_in,
           send_sem, recv_sem, hs_sem, hr_sem, load_sem, stage_sem, o_sem, out_sem):
    row = lax.axis_index("row")
    col = lax.axis_index("col")
    n_row, n_col = 4, 4
    core = row % 2
    bits = (row // 2, col % 2, col // 2)
    flip = ({"row": row + 2 - 4 * (row // 2), "col": col}, {"row": row, "col": col + 1 - 2 * (col % 2)}, {"row": row, "col": col + 2 - 4 * (col // 2)})
    mate = {"row": row + 1 - 2 * core, "col": col}
    halves = (r0, r1, r2, r3)

    def when(cond):
        return pl.when(cond)

    barrier = pltpu.get_barrier_semaphore()
    for dev in (mate,) + flip:
        pl.semaphore_signal(barrier, inc=1, device_id=dev, device_id_type=MESH)
    near = ((row > 0, {"row": row - 1, "col": col}), (row < n_row - 1, {"row": row + 1, "col": col}),
            (col > 0, {"row": row, "col": col - 1}), (col < n_col - 1, {"row": row, "col": col + 1}))
    for cond, dev in near:
        @when(cond)
        def _():
            pl.semaphore_signal(barrier, inc=1, device_id=dev, device_id_type=MESH)

    g_load = pltpu.make_async_copy(g_ref, gs.at[1, pl.ds(1, ROWS)], load_sem.at[0])
    g_load.start()
    w_load = pltpu.make_async_copy(w2_ref, wbuf, load_sem.at[1])

    def stage_copy(src, chunk, slot):
        return pltpu.make_async_copy(src.at[pl.ds(pl.multiple_of(chunk * GPIX, GPIX), GPIX)], stage.at[slot], stage_sem.at[slot])

    stage_copy(a_ref, 0, 0).start()

    @when(row == 0)
    def _():
        gs[1, 0] = jnp.zeros((COLS, CH), BF16)
        gs[3, 0] = jnp.zeros((COLS, CH), BF16)

    @when(row == n_row - 1)
    def _():
        gs[1, ROWS + 1] = jnp.zeros((COLS, CH), BF16)
        gs[3, ROWS + 1] = jnp.zeros((COLS, CH), BF16)

    @when(col == 0)
    def _():
        for u in range(2):
            edge_in[u, 0] = jnp.zeros((32, CH), F32)

    @when(col == n_col - 1)
    def _():
        for u in range(2):
            edge_in[u, 1] = jnp.zeros((32, CH), F32)

    for u in range(2):
        for v in range(2):
            edge_out[u, v, 24:32] = jnp.zeros((8, CH), F32)

    pl.semaphore_wait(barrier, 8 - row // 3 - (3 - row) // 3 - col // 3 - (3 - col) // 3)

    def row_copy(u, plane, down, src=None):
        src_row, dst_row = (ROWS, 0) if down else (1, ROWS + 1)
        dev = {"row": row + 1, "col": col} if down else {"row": row - 1, "col": col}
        n = u * 4 + (0 if down else 1)
        source = gs.at[plane, src_row] if src is None else src.at[src_row - 1]
        return pltpu.make_async_remote_copy(source, gs.at[plane, dst_row], hs_sem.at[n], hr_sem.at[n], device_id=dev, device_id_type=MESH)

    def col_copy(u, right):
        dev = {"row": row, "col": col + 1} if right else {"row": row, "col": col - 1}
        n = u * 4 + (2 if right else 3)
        a, b = (1, 0) if right else (0, 1)
        return pltpu.make_async_remote_copy(edge_out.at[u, a], edge_in.at[u, b], hs_sem.at[n], hr_sem.at[n], device_id=dev, device_id_type=MESH)

    def send_rows(u, plane, src=None):
        @when(row < n_row - 1)
        def _():
            row_copy(u, plane, True, src).start()

        @when(row > 0)
        def _():
            row_copy(u, plane, False, src).start()

    def wait_rows(u, plane, src=None):
        @when(row > 0)
        def _():
            row_copy(u, plane, True, src).wait_recv()
            row_copy(u, plane, False, src).wait_send()

        @when(row < n_row - 1)
        def _():
            row_copy(u, plane, False, src).wait_recv()
            row_copy(u, plane, True, src).wait_send()

    def send_cols(u, plane):
        def body(r, _):
            edge_out[u, 0, pl.ds(r, 1)] = gs[plane, r, 0:16].astype(F32)[0:1]
            edge_out[u, 1, pl.ds(r, 1)] = gs[plane, r, COLS - 16:COLS].astype(F32)[15:16]
            return 0

        lax.fori_loop(0, ROWS + 2, body, 0)

        @when(col < n_col - 1)
        def _():
            col_copy(u, True).start()

        @when(col > 0)
        def _():
            col_copy(u, False).start()

    def wait_cols(u):
        @when(col > 0)
        def _():
            col_copy(u, True).wait_recv()
            col_copy(u, False).wait_send()

        @when(col < n_col - 1)
        def _():
            col_copy(u, False).wait_recv()
            col_copy(u, True).wait_send()

    def build_shifts(u, plane):
        spot = lax.broadcasted_iota(jnp.int32, (COLS, CH), 0)

        def body(r, _):
            val = gs[plane, r].astype(F32)
            left = edge_in[u, 0, pl.ds(r, 1)]
            right = edge_in[u, 1, pl.ds(r, 1)]
            gs[0, r] = jnp.where(spot == 0, left, pltpu.roll(val, 1, 0)).astype(BF16)
            gs[2, r] = jnp.where(spot == COLS - 1, right, pltpu.roll(val, COLS - 1, 0)).astype(BF16)
            return 0

        lax.fori_loop(0, ROWS + 2, body, 0)

    def transpose_in(src, act):
        def body(chunk, _):
            slot = chunk % 2

            @when(chunk + 1 < NGROUP)
            def _():
                stage_copy(src, chunk + 1, 1 - slot).start()

            stage_copy(src, chunk, slot).wait()
            for j in range(GPIX // 256):
                val = stage[slot, j * 256:(j + 1) * 256]
                if act:
                    val = gelu_val(val.astype(F32)).astype(BF16)
                lhs_t[:, pl.ds(pl.multiple_of(chunk * GPIX + j * 256, 256), 256)] = val.T
            return 0

        lax.fori_loop(0, NGROUP, body, 0)

    def base_of(t, level):
        off = core * 256
        for n in range(level):
            off = off + bits[(t + n) % 3] * HALVES[n + 1]
        return off

    def axis_of(t, level):
        return mate if level == 0 else flip[(t + level - 1) % 3]

    def reduce_copy(t, level, core_off=None):
        size = HALVES[level]
        if level == 0:
            off = (1 - core) * 256
        else:
            off = base_of(t, level - 1) + (1 - bits[(t + level - 1) % 3]) * size
        off = pl.multiple_of(off, 32)
        return pltpu.make_async_remote_copy(part.at[t, pl.ds(off, size)], halves[level].at[t], send_sem.at[t, level], recv_sem.at[t, level], device_id=axis_of(t, level), device_id_type=MESH)

    def gather_copy(t, level):
        size = HALVES[level]
        off = pl.multiple_of(base_of(t, level), 32)
        n = 7 - level
        return pltpu.make_async_remote_copy(full.at[t, pl.ds(off, size)], full.at[t, pl.ds(off, size)], send_sem.at[t, n], recv_sem.at[t, n], device_id=axis_of(t, level), device_id_type=MESH)

    def result_copy(w, t):
        tap = order_of(t)[2]
        return pltpu.make_async_copy(full.at[t], (dw2_ref, dw1_ref)[w].at[tap], out_sem.at[t])

    def event(w, t, s):
        if s <= 3:
            reduce_copy(t, s).wait_recv()
            size = HALVES[s]
            rows = pl.ds(pl.multiple_of(base_of(t, s), 32), size)
            (part if s < 3 else full)[t, rows] = part[t, rows] + halves[s][t]
            (reduce_copy(t, s + 1) if s < 3 else gather_copy(t, 3)).start()
        else:
            gather_copy(t, 7 - s).wait_recv()
            if s < 7:
                gather_copy(t, 6 - s).start()
            else:
                for level in range(4):
                    reduce_copy(t, level).wait_send()
                    gather_copy(t, level).wait_send()
                result_copy(w, t).start()

    def pump(i, base, count):
        for n in range(count):
            if slots[base + n]:
                @when(i == n)
                def _():
                    for w, t, s in slots[base + n]:
                        event(w, t, s)

    def tap_sum(i, plane):
        row_at = (i % 3 + 1) % 3
        grad = gs[plane, pl.ds(row_at, ROWS)].reshape(PIX, CH)
        part[i] = jnp.dot(lhs_t[...], grad, preferred_element_type=F32)
        pltpu.make_async_remote_copy(part.at[i, pl.ds(pl.multiple_of((1 - core) * 256, 256), 256)], r0.at[i], send_sem.at[i, 0], recv_sem.at[i, 0], device_id=mate, device_id_type=MESH).start()

    def conv_rows(g, center):
        top = g * GROUP
        lhs = []
        rhs = []
        for k in range(9):
            a, c = k // 3, k % 3
            plane = (0, center, 2)[2 - c]
            lhs.append(gs[plane, pl.ds(top + 2 - a, GROUP)].reshape(GPIX, CH))
            rhs.append(wbuf[k])
        return lax.dot_general(jnp.concatenate(lhs, axis=1), jnp.concatenate(rhs, axis=1), (((1,), (1,)), ((), ())), preferred_element_type=F32)

    send_rows(0, 1, g_ref)
    w_load.start()
    transpose_in(a_ref, True)
    g_load.wait()
    wait_rows(0, 1, g_ref)
    send_cols(0, 1)

    def w2_step(i, _):
        @when(i == 3)
        def _():
            wait_cols(0)
            build_shifts(0, 1)

        tap_sum(i, (i // 3 + 1) % 3)
        pump(i, 0, 9)
        return 0

    lax.fori_loop(0, 9, w2_step, 0)

    w_load.wait()

    def group_of(gi):
        return jnp.where(gi == 0, 0, jnp.where(gi == 1, NGROUP - 1, gi - 1))

    stage_copy(a_ref, 0, 0).start()

    def dz_step(gi, _):
        g = group_of(gi)
        slot = gi % 2

        @when(gi + 1 < NGROUP)
        def _():
            stage_copy(a_ref, group_of(gi + 1), 1 - slot).start()

        d_z = conv_rows(g, 1)
        stage_copy(a_ref, g, slot).wait()
        d_a = (d_z * gelu_slope(stage[slot].astype(F32))).astype(BF16)
        gs[3, pl.ds(g * GROUP + 1, GROUP)] = d_a.reshape(GROUP, COLS, CH)

        @when(gi == 1)
        def _():
            send_rows(1, 3)

        pump(gi, 9, NGROUP)
        return 0

    lax.fori_loop(0, NGROUP, dz_step, 0)
    w1_load = pltpu.make_async_copy(w1_ref, wbuf, load_sem.at[1])
    w1_load.start()
    stage_copy(x_ref, 0, 0).start()
    wait_rows(1, 3)
    send_cols(1, 3)
    transpose_in(x_ref, False)

    def w1_step(i, _):
        @when(i == 3)
        def _():
            wait_cols(1)
            build_shifts(1, 3)

        pltpu.make_async_copy(full.at[i], dw2_ref.at[0], out_sem.at[i]).wait()
        u = (i // 3 + 1) % 3
        tap_sum(i, u + 2 * u * (2 - u))
        pump(i, 15, 9)
        return 0

    lax.fori_loop(0, 9, w1_step, 0)

    w1_load.wait()

    def out_copy(g):
        return pltpu.make_async_copy(gs.at[1, pl.ds(g * GROUP + 1, GROUP)], dx_ref.at[pl.ds(g * GROUP, GROUP)], o_sem.at[g])

    def dx_step(g, _):
        rows = pl.ds(g * GROUP + 1, GROUP)
        val = conv_rows(g, 3) + gs[1, rows].reshape(GPIX, CH).astype(F32)
        gs[1, rows] = val.astype(BF16).reshape(GROUP, COLS, CH)
        out_copy(g).start()
        pump(g, 24, NGROUP)
        return 0

    lax.fori_loop(0, NGROUP, dx_step, 0)
    for w, t, s in slots[30]:
        event(w, t, s)
    for t in range(9):
        result_copy(1, t).wait()
    for g in range(NGROUP):
        out_copy(g).wait()


def solution(mesh):
    slots, _ = build_slots()

    def local_step(x_tile, a_tile, g_tile, w_one, w_two):
        any_spec = pl.BlockSpec(memory_space=pl.ANY)
        d_x, d_w1, d_w2 = pl.pallas_call(
            functools.partial(kernel, slots),
            out_shape=(jax.ShapeDtypeStruct((ROWS, COLS, CH), BF16), jax.ShapeDtypeStruct((9, CH, CH), F32), jax.ShapeDtypeStruct((9, CH, CH), F32)),
            in_specs=[any_spec] * 5,
            out_specs=[any_spec] * 3,
            scratch_shapes=[
                pltpu.VMEM((9, CH, CH), F32),
                pltpu.VMEM((9, CH, CH), F32),
                pltpu.VMEM((9, 256, CH), F32),
                pltpu.VMEM((9, 128, CH), F32),
                pltpu.VMEM((9, 64, CH), F32),
                pltpu.VMEM((9, 32, CH), F32),
                pltpu.VMEM((CH, PIX), BF16),
                pltpu.VMEM((4, ROWS + 2, COLS, CH), BF16),
                pltpu.VMEM((9, CH, CH), BF16),
                pltpu.VMEM((2, GPIX, CH), BF16),
                pltpu.VMEM((2, 2, 32, CH), F32),
                pltpu.VMEM((2, 2, 32, CH), F32),
                pltpu.SemaphoreType.DMA((9, 8)),
                pltpu.SemaphoreType.DMA((9, 8)),
                pltpu.SemaphoreType.DMA((8,)),
                pltpu.SemaphoreType.DMA((8,)),
                pltpu.SemaphoreType.DMA((2,)),
                pltpu.SemaphoreType.DMA((2,)),
                pltpu.SemaphoreType.DMA((NGROUP,)),
                pltpu.SemaphoreType.DMA((9,)),
            ],
            compiler_params=pltpu.CompilerParams(collective_id=0, has_side_effects=True, vmem_limit_bytes=67043328),
        )(x_tile.reshape(PIX, CH), a_tile.reshape(PIX, CH), g_tile.reshape(ROWS, COLS, CH), w_one.reshape(9, CH, CH), w_two.reshape(9, CH, CH))
        return d_x.reshape(1, ROWS, COLS, CH), d_w1.reshape(3, 3, CH, CH), d_w2.reshape(3, 3, CH, CH)

    tile_spec = P(None, "row", "col", None)
    return jax.shard_map(local_step, mesh=mesh, in_specs=(tile_spec, tile_spec, tile_spec, P(), P()), out_specs=(tile_spec, P(), P()), check_vma=False)
```

time: 434 us -> 197 us (0.45)
  Pallas kernels: 0 us -> 179 us
  matrix products: 133 us -> 0 us
  waiting for transfers between devices: 126 us -> 0 us
  local copies, waits for them, and re-layouts: 89.3 us -> 16.8 us
  other arithmetic: 44.3 us -> 0.01 us
  starting transfers between devices: 21.7 us -> 0 us
  between operations: 14.8 us -> 0.67 us
    pallas_call x0 -> x1, Pallas kernels: none -> 179 us  [local_step(): pl.pallas_call(functools.partial(kernel, slots), out_shape=(jax.ShapeDtyp...]
    psum x1 -> x0, waiting for transfers between devices: 126 us -> none  [local_step(): d_w1, d_w2 = lax.psum((w1_part, w2_part), ('row', 'col'))]
    dot_general x18 -> x0, matrix products: 81.2 us -> none  [tap_grads(): jnp.einsum('bhwi,bhwo->io', tile_in, grad_wide[:, 2 - tap_row:2 - tap_row...]
    conv_general_dilated x9 -> x0, local copies, waits for them, and re-layouts: 55.9 us -> none  [conv_valid(): lax.conv_general_dilated(lhs_arr, rhs_arr, (1, 1), 'VALID', dimension_num...]
    conv_general_dilated x2 -> x0, matrix products: 51.6 us -> none  [conv_valid(): lax.conv_general_dilated(lhs_arr, rhs_arr, (1, 1), 'VALID', dimension_num...]
    ppermute x8 -> x0, starting transfers between devices: 21.6 us -> none  [the longest x2 9.46 us: add_halo(): from_left = lax.ppermute(tall[:, :, -1:], 'col', col_down)]
    convert_element_type x2 -> x0, other arithmetic: 19.2 us -> none  [the longest x1 11.3 us: local_step(): d_a = (d_z * gelu_slope(a_val)).astype(jnp.bfloat16)]
    concatenate x3 -> x0, other arithmetic: 12.8 us -> none  [add_halo(): return jnp.concatenate([from_left, tall, from_right], axis=2)]
  transfers between devices with their start and end apart: 9 -> 0, of which waited for: 1 -> 0; matrix products, arithmetic and copies ran while one was open for 34% -> 0% of each run, Pallas kernels for 0% -> 0%
where the time goes in v1:
time: 197 us
  Pallas kernels  179 us (91%)
  local copies, waits for them, and re-layouts  16.8 us (9%)
    pallas_call x1, Pallas kernels, local_step(): pl.pallas_call(functools.partial(kernel, slots), out_shape=(jax.ShapeDtyp...  179 us
    unnamed x11, local copies, waits for them, and re-layouts  16.8 us

profile of v1, /device:TPU:0, one launch (start us, length us, event | category | flops | bytes accessed | tf_op | source)
XLA Modules:
  0.0 196.5 jit_solution(10794406528139848676)
XLA Ops:
  0.6 179.1 %shard_map.76 = (bf16[24,192,512]{2,1,0:T(8,128)(2,1)}, f32[9,512,512]{2,1,0:T(8,128)}, f32[9,512,512]{2,1,0:T(8,128)}) custom-call(bf16[4608,512]{1,0:T(8,128)(2,1)} %bitcast.13, bf16[4608,512]{1,0:T(8,128)(2,1)} %bitcast.14, bf16[24,192,512]{2,1,0:T(8,128)(2,1)} %bitcast.15, bf16[9,512,512]{2,1,0:T(8,128)(2,1)} %bitcast.16, bf16[9,512,512]{2,1,0:T(8,128)(2,1)} %bitcast.17), custom_call_target="tpu_custom_call" | custom-call | tf_op jit(solution)/shard_map/pallas_call | solution.py:416
  179.7 0.0 copy-start
  179.7 0.0 slice-start
  179.7 0.0 slice-start.1
  179.8 5.3 %copy.11 = bf16[1,24,192,512]{3,2,1,0:T(8,128)(2,1)} copy(bf16[1,24,192,512]{3,2,1,0:T(8,128)(2,1)} %bitcast.12) | data formatting | bytes 9437184
  185.1 1.4 copy-done
  186.5 0.0 slice-start.2
  186.5 4.8 %copy.12 = f32[3,3,512,512]{3,2,1,0:T(8,128)} copy(f32[3,3,512,512]{3,2,1,0:T(8,128)S(1)} %bitcast.11) | data formatting | bytes 18874368
  191.3 0.0 slice-done
  191.3 1.0 slice-done.1
  192.3 0.5 slice-done.2
  192.8 3.7 %copy.13 = f32[3,3,512,512]{3,2,1,0:T(8,128)} copy(f32[3,3,512,512]{3,2,1,0:T(8,128)S(1)} %bitcast.10) | data formatting | bytes 18874368
  (1 shorter events, 0.0 us)
Async XLA Ops:
  179.7 6.8 %copy-start = (f32[9,512,512]{2,1,0:T(8,128)S(1)}, f32[9,512,512]{2,1,0:T(8,128)}, u32[]{:S(2)}) copy-start(f32[9,512,512]{2,1,0:T(8,128)} %get-tuple-element.7) | copy-start | bytes 28311556
  179.7 11.6 %slice-start = ((s8[9437184]{0:T(1024)(128)(4,1)}), s8[4194304]{0:T(1024)(128)(4,1)S(1)}, s32[]{:S(2)}) async-start(s8[9437184]{0:T(1024)(128)(4,1)} %bitcast.8), calls=%async_computation | async-start | bytes 8388608
  179.7 12.6 %slice-start.1 = ((s8[9437184]{0:T(1024)(128)(4,1)}), s8[4194304]{0:T(1024)(128)(4,1)S(1)}, s32[]{:S(2)}) async-start(s8[9437184]{0:T(1024)(128)(4,1)} %bitcast.8), calls=%async_computation.1 | async-start | bytes 8388608
  186.5 6.3 %slice-start.2 = ((s8[9437184]{0:T(1024)(128)(4,1)}), s8[1048576]{0:T(1024)(128)(4,1)S(1)}, s32[]{:S(2)}) async-start(s8[9437184]{0:T(1024)(128)(4,1)} %bitcast.8), calls=%async_computation.2 | async-start | bytes 2097152

commit v2 on v0

v2 whole, which is shorter than its diff:
```python
import functools

import jax
import jax.numpy as jnp
from jax import lax
from jax.experimental import pallas as pl
from jax.experimental.pallas import tpu as pltpu
from jax.sharding import PartitionSpec as P

MESH = pl.DeviceIdType.MESH
F32 = jnp.float32
BF16 = jnp.bfloat16
ROWS, COLS, CH = 24, 192, 512
PIX = ROWS * COLS
GROUP = 2
GPIX = GROUP * COLS
NGROUP = ROWS // GROUP
HALVES = (256, 128, 64, 32)
PARTS = 2
WIDTH = CH // PARTS
SIDE = 256
ORDER = (4, 1, 7, 3, 0, 6, 5, 2, 8)


def build_slots(half=1.33, shift=2.4, dz=2.1, dx=2.0, halo=0.5, mid=0.6, first=12.7, rate=46.6, lat=2.3, hop=1.8):
    size = {1: 0.262144e3, 2: 0.131072e3, 3: 0.065536e3}
    add = (0.075, 0.04, 0.02, 0.01)
    link = [0.0, 0.0, 0.0]
    arrive = {}

    def send(now, w, t, j, s):
        if s in (0, 7):
            arrive[(w, t, j, s)] = now + hop * (0.6 + 0.4 / PARTS)
            return
        level = s if s <= 3 else 7 - s
        axis = (t + j + level - 1) % 3
        link[axis] = max(now, link[axis]) + size[level] / PARTS / rate
        arrive[(w, t, j, s)] = link[axis] + lat

    def handle(now, key):
        del arrive[key]
        w, t, j, s = key
        now += 0.03 + (add[s] / PARTS if s < 4 else 0.0)
        if s < 7:
            send(now, w, t, j, s + 1)
        return now

    steps = []
    for w in range(2):
        for n in range(18):
            steps.append((half + (shift if n == 6 else 0.0) + (halo if w and n == 0 else 0.0), (w, n)))
        steps += [((dx if w else dz), None)] * NGROUP
    now = first
    slots = []
    for index, (length, made) in enumerate(steps):
        if index == 18 + NGROUP:
            now += mid
        if made is not None and made[0] == 1 and made[1] % 2 == 0:
            while any(k[0] == 0 and k[1] == made[1] // 2 for k in arrive):
                when, key = min((v, k) for k, v in arrive.items())
                now = handle(max(now, when), key)
                slots[-1].append(key)
        now += length
        if made is not None and made[1] % 2 == 0:
            for j in range(PARTS):
                send(now + 0.1, made[0], made[1] // 2, j, 0)
        here = []
        while True:
            ready = [(k[3], v, k) for k, v in arrive.items() if v <= now and not (k[3] == 0 and made is not None and made[1] % 2 == 0 and made[1] // 2 == k[1])]
            if not ready:
                break
            key = min(ready)[2]
            now = handle(now, key)
            here.append(key)
        slots.append(here)
    tail = []
    while arrive:
        now = max(now, min(arrive.values()))
        key = min((k[3], v, k) for k, v in arrive.items() if v <= now)[2]
        now = handle(now, key)
        tail.append(key)
    slots.append(tail)
    return slots, now


def gelu_val(a):
    return a * (0.5 * (1.0 + jnp.tanh(0.7978845608028654 * (a + 0.044715 * (a * a * a)))))


def gelu_slope(a):
    t = jnp.tanh(0.7978845608028654 * (a + 0.044715 * a * a * a))
    return 0.5 * (1.0 + t) + 0.5 * a * (1.0 - t * t) * 0.7978845608028654 * (1.0 + 3.0 * 0.044715 * a * a)


def kernel(slots, x_ref, a_ref, g_ref, w1_ref, w2_ref, lv, full, dw2_ref,
           part, r0, r1, r2, r3, mid, dc, sh, wbuf, stage, dzs, edge_out, edge_in,
           send_sem, recv_sem, hs_sem, hr_sem, load_sem, stage_sem, out_sem):
    row = lax.axis_index("row")
    col = lax.axis_index("col")
    n_row, n_col = 4, 4
    core = row % 2
    bits = (row // 2, col % 2, col // 2)
    flip = ({"row": row + 2 - 4 * (row // 2), "col": col}, {"row": row, "col": col + 1 - 2 * (col % 2)}, {"row": row, "col": col + 2 - 4 * (col // 2)})
    mate = {"row": row + 1 - 2 * core, "col": col}
    halves = (r0, r1, r2, r3)

    barrier = pltpu.get_barrier_semaphore()
    for dev in (mate,) + flip:
        pl.semaphore_signal(barrier, inc=1, device_id=dev, device_id_type=MESH)
    near = ((row > 0, {"row": row - 1, "col": col}), (row < n_row - 1, {"row": row + 1, "col": col}),
            (col > 0, {"row": row, "col": col - 1}), (col < n_col - 1, {"row": row, "col": col + 1}))
    for cond, dev in near:
        @pl.when(cond)
        def _():
            pl.semaphore_signal(barrier, inc=1, device_id=dev, device_id_type=MESH)

    chunk = ROWS // 3
    a_loads = [pltpu.make_async_copy(a_ref.at[pl.ds(n * chunk, chunk)], sh.at[0, pl.ds(n * chunk, chunk)], load_sem.at[2 + n]) for n in range(3)]
    g_load = pltpu.make_async_copy(g_ref, mid.at[pl.ds(1, ROWS)], load_sem.at[0])
    w_load = pltpu.make_async_copy(w2_ref, wbuf, load_sem.at[1])
    for copy in a_loads + [g_load, w_load]:
        copy.start()

    @pl.when(row == 0)
    def _():
        mid[0] = jnp.zeros((COLS, CH), BF16)
        dc[0] = jnp.zeros((COLS, CH), BF16)

    @pl.when(row == n_row - 1)
    def _():
        mid[ROWS + 1] = jnp.zeros((COLS, CH), BF16)
        dc[ROWS + 1] = jnp.zeros((COLS, CH), BF16)

    @pl.when(col == 0)
    def _():
        for u in range(2):
            edge_in[u, 0] = jnp.zeros((32, CH), F32)

    @pl.when(col == n_col - 1)
    def _():
        for u in range(2):
            edge_in[u, 1] = jnp.zeros((32, CH), F32)

    for u in range(2):
        for v in range(2):
            edge_out[u, v, 24:32] = jnp.zeros((8, CH), F32)

    centers = (mid, dc)

    def row_copy(u, down):
        src_row, dst_row = (ROWS, 0) if down else (1, ROWS + 1)
        dev = {"row": row + 1, "col": col} if down else {"row": row - 1, "col": col}
        n = u * 4 + (0 if down else 1)
        source = dc.at[src_row] if u else g_ref.at[src_row - 1]
        return pltpu.make_async_remote_copy(source, centers[u].at[dst_row], hs_sem.at[n], hr_sem.at[n], device_id=dev, device_id_type=MESH)

    def col_copy(u, right):
        dev = {"row": row, "col": col + 1} if right else {"row": row, "col": col - 1}
        n = u * 4 + (2 if right else 3)
        a, b = (1, 0) if right else (0, 1)
        return pltpu.make_async_remote_copy(edge_out.at[u, a], edge_in.at[u, b], hs_sem.at[n], hr_sem.at[n], device_id=dev, device_id_type=MESH)

    def send_rows(u):
        @pl.when(row < n_row - 1)
        def _():
            row_copy(u, True).start()

        @pl.when(row > 0)
        def _():
            row_copy(u, False).start()

    def wait_rows(u):
        @pl.when(row > 0)
        def _():
            row_copy(u, True).wait_recv()
            row_copy(u, False).wait_send()

        @pl.when(row < n_row - 1)
        def _():
            row_copy(u, False).wait_recv()
            row_copy(u, True).wait_send()

    def send_cols(u):
        def body(r, _):
            edge_out[u, 0, pl.ds(r, 1)] = centers[u][r, 0:16].astype(F32)[0:1]
            edge_out[u, 1, pl.ds(r, 1)] = centers[u][r, COLS - 16:COLS].astype(F32)[15:16]
            return 0

        lax.fori_loop(0, ROWS + 2, body, 0)

        @pl.when(col < n_col - 1)
        def _():
            col_copy(u, True).start()

        @pl.when(col > 0)
        def _():
            col_copy(u, False).start()

    def wait_cols(u):
        @pl.when(col > 0)
        def _():
            col_copy(u, True).wait_recv()
            col_copy(u, False).wait_send()

        @pl.when(col < n_col - 1)
        def _():
            col_copy(u, False).wait_recv()
            col_copy(u, True).wait_send()

    def build_shifts(u):
        spot = lax.broadcasted_iota(jnp.int32, (COLS, CH), 0)

        def body(r, _):
            val = centers[u][r].astype(F32)
            left = edge_in[u, 0, pl.ds(r, 1)]
            right = edge_in[u, 1, pl.ds(r, 1)]
            sh[0, r] = jnp.where(spot == 0, left, pltpu.roll(val, 1, 0)).astype(BF16)
            sh[1, r] = jnp.where(spot == COLS - 1, right, pltpu.roll(val, COLS - 1, 0)).astype(BF16)
            return 0

        lax.fori_loop(0, ROWS + 2, body, 0)

    def base_of(rot, level):
        off = core * 256
        for n in range(level):
            off = off + bits[(rot + n) % 3] * HALVES[n + 1]
        return off

    def axis_of(rot, level):
        return mate if level == 0 else flip[(rot + level - 1) % 3]

    def reduce_copy(t, j, level, tap=None):
        rot = t + j
        tap = ORDER[t] if tap is None else tap
        size = HALVES[level]
        if level == 0:
            off = (1 - core) * 256
        else:
            off = base_of(rot, level - 1) + (1 - bits[(rot + level - 1) % 3]) * size
        rows, cols = pl.ds(pl.multiple_of(off, 32), size), pl.ds(j * WIDTH, WIDTH)
        return pltpu.make_async_remote_copy(part.at[tap, rows, cols], halves[level].at[tap, :, cols], send_sem.at[tap, j, level], recv_sem.at[tap, j, level], device_id=axis_of(rot, level), device_id_type=MESH)

    def gather_copy(t, j, level):
        rot, tap = t + j, ORDER[t]
        view = full.at[tap, pl.ds(pl.multiple_of(base_of(rot, level), 32), HALVES[level]), pl.ds(j * WIDTH, WIDTH)]
        n = 7 - level
        return pltpu.make_async_remote_copy(view, view, send_sem.at[tap, j, n], recv_sem.at[tap, j, n], device_id=axis_of(rot, level), device_id_type=MESH)

    def result_copy(tap, j):
        cols = pl.ds(j * WIDTH, WIDTH)
        return pltpu.make_async_copy(full.at[tap, :, cols], dw2_ref.at[tap, :, cols], out_sem.at[tap, j])

    def event(w, t, j, s):
        if s <= 3:
            reduce_copy(t, j, s).wait_recv()
            tap, cols = ORDER[t], slice(j * WIDTH, (j + 1) * WIDTH)
            rows = pl.ds(pl.multiple_of(base_of(t + j, s), 32), HALVES[s])
            (part if s < 3 else full)[tap, rows, cols] = part[tap, rows, cols] + halves[s][tap, :, cols]
            (reduce_copy(t, j, s + 1) if s < 3 else gather_copy(t, j, 3)).start()
        else:
            gather_copy(t, j, 7 - s).wait_recv()
            if s < 7:
                gather_copy(t, j, 6 - s).start()
            else:
                for level in range(4):
                    reduce_copy(t, j, level).wait_send()
                    gather_copy(t, j, level).wait_send()
                if w == 0:
                    result_copy(ORDER[t], j).start()

    def pump(n, base, lo, hi):
        if not any(slots[base + m] for m in range(lo, hi)):
            return
        if hi - lo == 1:
            for key in slots[base + lo]:
                event(*key)
            return
        half = (lo + hi) // 2

        @pl.when(n < half)
        def _():
            pump(n, base, lo, half)

        @pl.when(n >= half)
        def _():
            pump(n, base, half, hi)

    def tap_half(n, tap, row_at, plane):
        second = n % 2
        rows = pl.ds(pl.multiple_of(core * 256 + (1 - second) * (1 - 2 * core) * 256, 256), 256)
        grad = plane[pl.ds(row_at, ROWS)].reshape(PIX, CH)
        part[tap, rows] = lax.dot_general(lv[:, rows], grad, (((0,), (0,)), ((), ())), preferred_element_type=F32)

        @pl.when(second == 0)
        def _():
            for j in range(PARTS):
                reduce_copy(0, j, 0, tap).start()

    def free_tap(n, tap, again):
        if again:
            @pl.when(n % 2 == 0)
            def _():
                for j in range(PARTS):
                    result_copy(tap, j).wait()

    def tap_loops(u, base):
        def middle(n, _):
            @pl.when(n == 2)
            def _():
                if u == 0:
                    wait_rows(0)
                    send_cols(0)

            row_at = (n // 2 + 1) % 3
            tap = (2 - row_at) * 3 + 1
            free_tap(n, tap, u)
            tap_half(n, tap, row_at, centers[u])
            pump(n, base, 0, 6)
            return 0

        def side(n, _):
            which = n // 6
            row_at = (n // 2 % 3 + 1) % 3
            tap = (2 - row_at) * 3 + 2 * which
            free_tap(n, tap, u)
            tap_half(n, tap, row_at, sh.at[1 - which])
            pump(n, base + 6, 0, 12)
            return 0

        lax.fori_loop(0, 6, middle, 0)
        wait_cols(u)
        build_shifts(u)
        lax.fori_loop(0, 12, side, 0)

    def conv_rows(g, center):
        lhs = []
        rhs = []
        for k in range(9):
            a, c = k // 3, k % 3
            plane = (sh.at[1], center, sh.at[0])[c]
            lhs.append(plane[pl.ds(g * GROUP + 2 - a, GROUP)].reshape(GPIX, CH))
            rhs.append(wbuf[k])
        return lax.dot_general(jnp.concatenate(lhs, axis=1), jnp.concatenate(rhs, axis=1), (((1,), (1,)), ((), ())), preferred_element_type=F32)

    for n in range(3):
        a_loads[n].wait()

        def gelu_row(r, _):
            lv[pl.ds(pl.multiple_of(r * COLS, COLS), COLS)] = gelu_val(sh[0, r].astype(F32)).astype(BF16)
            return 0

        lax.fori_loop(n * chunk, (n + 1) * chunk, gelu_row, 0)
        if n == 0:
            pl.semaphore_wait(barrier, 8 - row // 3 - (3 - row) // 3 - col // 3 - (3 - col) // 3)
            send_rows(0)
    g_load.wait()

    tap_loops(0, 0)

    x_load = pltpu.make_async_copy(x_ref, lv, load_sem.at[0])
    x_load.start()
    w_load.wait()

    def group_of(gi):
        return jnp.where(gi == 0, 0, jnp.where(gi == 1, NGROUP - 1, gi - 1))

    def stage_copy(gi, slot):
        return pltpu.make_async_copy(a_ref.at[pl.ds(group_of(gi) * GROUP, GROUP)], stage.at[slot], stage_sem.at[slot])

    def slope_rows(gi, slot):
        a_val = stage[slot].reshape(GPIX, CH).astype(F32)
        d_a = (dzs[...] * gelu_slope(a_val)).astype(BF16)
        dc[pl.ds(group_of(gi) * GROUP + 1, GROUP)] = d_a.reshape(GROUP, COLS, CH)

    stage_copy(0, 0).start()
    dzs[...] = jnp.zeros((GPIX, CH), F32)
    stage_copy(0, 0).wait()

    def dz_step(gi, _):
        before = jnp.maximum(gi - 1, 0)
        slot = before % 2

        @pl.when(gi >= 2)
        def _():
            stage_copy(before, slot).wait()

        @pl.when(gi >= 1)
        def _():
            stage_copy(gi, gi % 2).start()

        slope_rows(before, slot)
        dzs[...] = conv_rows(group_of(gi), mid)

        @pl.when(gi == 2)
        def _():
            send_rows(1)

        pump(gi, 18, 0, NGROUP)
        return 0

    lax.fori_loop(0, NGROUP, dz_step, 0)
    w1_load = pltpu.make_async_copy(w1_ref, wbuf, load_sem.at[1])
    w1_load.start()
    stage_copy(NGROUP - 1, (NGROUP - 1) % 2).wait()
    slope_rows(NGROUP - 1, (NGROUP - 1) % 2)
    wait_rows(1)
    send_cols(1)
    x_load.wait()

    tap_loops(1, 18 + NGROUP)

    w1_load.wait()

    def dx_step(g, _):
        val = conv_rows(g, dc) + mid[pl.ds(g * GROUP + 1, GROUP)].reshape(GPIX, CH).astype(F32)
        lv[pl.ds(pl.multiple_of(g * GPIX, GPIX), GPIX)] = val.astype(BF16)
        pump(g, 36 + NGROUP, 0, NGROUP)
        return 0

    lax.fori_loop(0, NGROUP, dx_step, 0)
    for key in slots[36 + 2 * NGROUP]:
        event(*key)


def write_out(lv, full, dw2_in, dx_ref, dw1_ref, dw2_ref, bounce, in_sem, out_sem):
    reads = [pltpu.make_async_copy(dw2_in.at[k], bounce.at[k], in_sem.at[k]) for k in range(9)]
    writes = [pltpu.make_async_copy(bounce.at[k], dw2_ref.at[k], out_sem.at[k]) for k in range(9)]
    writes += [pltpu.make_async_copy(full.at[k], dw1_ref.at[k], out_sem.at[9 + k]) for k in range(9)]
    writes.append(pltpu.make_async_copy(lv, dx_ref, out_sem.at[18]))
    for copy in reads + writes[9:]:
        copy.start()
    for k in range(9):
        reads[k].wait()
        writes[k].start()
    for copy in writes:
        copy.wait()


def solution(mesh):
    slots, _ = build_slots()
    any_spec = pl.BlockSpec(memory_space=pl.ANY)
    vmem_spec = pl.BlockSpec(memory_space=pltpu.VMEM)

    def local_step(x_tile, a_tile, g_tile, w_one, w_two):
        lv, full, d_w2 = pl.pallas_call(
            functools.partial(kernel, slots),
            out_shape=(pltpu.VMEM((PIX, CH), BF16), pltpu.VMEM((9, CH, CH), F32), jax.ShapeDtypeStruct((9, CH, CH), F32)),
            in_specs=[any_spec] * 5,
            out_specs=(vmem_spec, vmem_spec, any_spec),
            scratch_shapes=[
                pltpu.VMEM((9, CH, CH), F32),
                pltpu.VMEM((9, 256, CH), F32),
                pltpu.VMEM((9, 128, CH), F32),
                pltpu.VMEM((9, 64, CH), F32),
                pltpu.VMEM((9, 32, CH), F32),
                pltpu.VMEM((ROWS + 2, COLS, CH), BF16),
                pltpu.VMEM((ROWS + 2, COLS, CH), BF16),
                pltpu.VMEM((2, ROWS + 2, COLS, CH), BF16),
                pltpu.VMEM((9, CH, CH), BF16),
                pltpu.VMEM((2, GROUP, COLS, CH), BF16),
                pltpu.VMEM((GPIX, CH), F32),
                pltpu.VMEM((2, 2, 32, CH), F32),
                pltpu.VMEM((2, 2, 32, CH), F32),
                pltpu.SemaphoreType.DMA((9, PARTS, 8)),
                pltpu.SemaphoreType.DMA((9, PARTS, 8)),
                pltpu.SemaphoreType.DMA((8,)),
                pltpu.SemaphoreType.DMA((8,)),
                pltpu.SemaphoreType.DMA((5,)),
                pltpu.SemaphoreType.DMA((2,)),
                pltpu.SemaphoreType.DMA((9, PARTS)),
            ],
            compiler_params=pltpu.CompilerParams(collective_id=0, has_side_effects=True, vmem_limit_bytes=52500000),
        )(x_tile.reshape(PIX, CH), a_tile.reshape(ROWS, COLS, CH), g_tile.reshape(ROWS, COLS, CH), w_one.reshape(9, CH, CH), w_two.reshape(9, CH, CH))
        d_x, d_w1, d_w2 = pl.pallas_call(
            write_out,
            out_shape=(jax.ShapeDtypeStruct((PIX, CH), BF16), jax.ShapeDtypeStruct((9, CH, CH), F32), jax.ShapeDtypeStruct((9, CH, CH), F32)),
            in_specs=[vmem_spec, vmem_spec, any_spec],
            out_specs=[any_spec] * 3,
            scratch_shapes=[pltpu.VMEM((9, CH, CH), F32), pltpu.SemaphoreType.DMA((9,)), pltpu.SemaphoreType.DMA((19,))],
            compiler_params=pltpu.CompilerParams(vmem_limit_bytes=50000000),
        )(lv, full, d_w2)
        return d_x.reshape(1, ROWS, COLS, CH), d_w1.reshape(3, 3, CH, CH), d_w2.reshape(3, 3, CH, CH)

    tile_spec = P(None, "row", "col", None)
    return jax.shard_map(local_step, mesh=mesh, in_specs=(tile_spec, tile_spec, tile_spec, P(), P()), out_specs=(tile_spec, P(), P()), check_vma=False)
```

time: 434 us -> 173 us (0.40)
  Pallas kernels: 0 us -> 168 us
  matrix products: 133 us -> 0 us
  waiting for transfers between devices: 126 us -> 0 us
  local copies, waits for them, and re-layouts: 89.3 us -> 3.63 us
  other arithmetic: 44.3 us -> 0 us
  starting transfers between devices: 21.7 us -> 0 us
  between operations: 14.8 us -> 0.65 us
    pallas_call x0 -> x2, Pallas kernels: none -> 168 us  [the longest x1 153 us: local_step(): pl.pallas_call(functools.partial(kernel, slots), out_shape=(pltpu.VMEM((P...]
    psum x1 -> x0, waiting for transfers between devices: 126 us -> none  [local_step(): d_w1, d_w2 = lax.psum((w1_part, w2_part), ('row', 'col'))]
    dot_general x18 -> x0, matrix products: 81.2 us -> none  [tap_grads(): jnp.einsum('bhwi,bhwo->io', tile_in, grad_wide[:, 2 - tap_row:2 - tap_row...]
    conv_general_dilated x9 -> x0, local copies, waits for them, and re-layouts: 55.9 us -> none  [conv_valid(): lax.conv_general_dilated(lhs_arr, rhs_arr, (1, 1), 'VALID', dimension_num...]
    conv_general_dilated x2 -> x0, matrix products: 51.6 us -> none  [conv_valid(): lax.conv_general_dilated(lhs_arr, rhs_arr, (1, 1), 'VALID', dimension_num...]
    unnamed x49 -> x2, local copies, waits for them, and re-layouts: 25.9 us -> 3.63 us
    ppermute x8 -> x0, starting transfers between devices: 21.6 us -> none  [the longest x2 9.46 us: add_halo(): from_left = lax.ppermute(tall[:, :, -1:], 'col', col_down)]
    convert_element_type x2 -> x0, other arithmetic: 19.2 us -> none  [the longest x1 11.3 us: local_step(): d_a = (d_z * gelu_slope(a_val)).astype(jnp.bfloat16)]
  transfers between devices with their start and end apart: 9 -> 0, of which waited for: 1 -> 0; matrix products, arithmetic and copies ran while one was open for 34% -> 0% of each run, Pallas kernels for 0% -> 0%
where the time goes in v2:
time: 173 us; the launch traced here: 172 us
  Pallas kernels  168 us (97%)
  local copies, waits for them, and re-layouts  3.63 us (2%)
    pallas_call x1, Pallas kernels, local_step(): pl.pallas_call(functools.partial(kernel, slots), out_shape=(pltpu.VMEM((P...  153 us
    pallas_call x1, Pallas kernels, local_step(): pl.pallas_call(write_out, out_shape=(jax.ShapeDtypeStruct((PIX, CH), BF16...  15.1 us
    unnamed x2, local copies, waits for them, and re-layouts  3.63 us

profile of v2, /device:TPU:0, one launch (start us, length us, event | category | flops | bytes accessed | tf_op | source)
XLA Modules:
  0.0 172.4 jit_solution(12806738338256809133)
XLA Ops:
  0.6 153.0 %shard_map.76 = (bf16[4608,512]{1,0:T(8,128)(2,1)S(1)}, f32[9,512,512]{2,1,0:T(8,128)S(1)}, f32[9,512,512]{2,1,0:T(8,128)}) custom-call(bf16[4608,512]{1,0:T(8,128)(2,1)} %bitcast.8, bf16[24,192,512]{2,1,0:T(8,128)(2,1)} %bitcast.9, bf16[24,192,512]{2,1,0:T(8,128)(2,1)} %bitcast.10, bf16[9,512,512]{2,1,0:T(8,128)(2,1)} %bitcast.11, bf16[9,512,512]{2,1,0:T(8,128)(2,1)} %bitcast.12), custom_call_target="tpu_custom_call" | custom-call | tf_op jit(solution)/shard_map/pallas_call | solution.py:445
  153.6 0.0 copy-start
  153.6 3.6 %copy-done = f32[9,512,512]{2,1,0:T(8,128)} copy-done((f32[9,512,512]{2,1,0:T(8,128)}, f32[9,512,512]{2,1,0:T(8,128)S(1)}, u32[]{:S(2)}) %copy-start) | copy-done | bytes 9437208
  157.3 15.1 %shard_map.77 = (bf16[4608,512]{1,0:T(8,128)(2,1)}, f32[9,512,512]{2,1,0:T(8,128)}, f32[9,512,512]{2,1,0:T(8,128)}) custom-call(bf16[4608,512]{1,0:T(8,128)(2,1)S(1)} %get-tuple-element.9.lv, f32[9,512,512]{2,1,0:T(8,128)} %copy-done, f32[9,512,512]{2,1,0:T(8,128)} %get-tuple-element.11.dw2_in), custom_call_target="tpu_custom_call" | custom-call | tf_op jit(solution)/shard_map/pallas_call | solution.py:474
Async XLA Ops:
  153.6 3.6 %copy-start = (f32[9,512,512]{2,1,0:T(8,128)}, f32[9,512,512]{2,1,0:T(8,128)S(1)}, u32[]{:S(2)}) copy-start(f32[9,512,512]{2,1,0:T(8,128)S(1)} %get-tuple-element.10.full) | copy-start | bytes 28311556
